TPU v7x, 1024 devices: a whole 4x4x32 slice. The times are simulated.
1024 devices in a mesh: row: 8 (over y, core), col: 16 (over z_lo), layer: 8 (over z_hi, x).
Axes of the slice: x: 4, y: 4, z: 32 (z_hi: 2, z_lo: 16; z = z_hi * 16 + z_lo), core: 2. Of those that a mesh axis runs over, the one named last changes fastest.
Arguments:
- a_values: bfloat16 [8, 8, 16, 2, 256, 256], P('row', 'layer', 'col'), may hold values from -0.375 to 0.375
- a_index: int32 [8, 8, 16, 2, 2], P('row', 'layer', 'col'), may hold values from 0 to 15, as said below
- a_count: int32 [8, 8, 16], P('row', 'layer', 'col'), may hold values from 0 to 2, as said below
- b_values: bfloat16 [8, 8, 16, 256, 2, 256], P('layer', 'row', 'col'), may hold values from -6 to 6
- b_index: int32 [8, 8, 16, 2, 2], P('layer', 'row', 'col'), may hold values from 0 to 7, as said below
- b_count: int32 [8, 8, 16], P('layer', 'row', 'col'), may hold values from 0 to 2, as said below
- c_index: int32 [8, 16, 2, 16], P('row', 'col'), may hold values from 0 to 15, as said below
- c_count: int32 [8, 16], P('row', 'col'), may hold values from 0 to 16, as said below
Outputs:
- c_blocks: float32 [8, 16, 16, 256, 256], P('row', 'col', 'layer')
Inputs may be any that keep to these rules, and one draw needn't show every extreme that they name: a_count is at most 2 and equals it for some tile; the first a_count slots of a tile name distinct blocks; each block row of A has exactly 1 stored blocks in every inner range. `a_index`: row entries lie below 16, inner entries below 1. b_count is at most 2 and equals it for some tile; the first b_count slots of a tile name distinct blocks; each block column of B has either no stored block or exactly 1 stored blocks in every inner range. `b_index`: inner entries lie below 2, column entries below 8. c_count is at most 16 and equals it for some tile; the first c_count slots of a tile name distinct blocks; the target pattern is exactly the set of blocks that the product A B reaches, and each of them receives exactly 1 block products in every inner range. `c_index`: row entries lie below 16, column entries below 8.
All inputs are finite; a program needn't handle non-finite values.
Results may differ from a plain program's by a relative error of at most 0.01.
Values may be sent and summed in bfloat16 or wider, within the bound.
A program may use at most 64 MiB of HBM per device.

v0:
```python
import functools

import jax
import jax.numpy as jnp
from jax import lax
from jax.experimental import pallas as pl
from jax.experimental.pallas import tpu as pltpu
from jax.sharding import Mesh
from jax.sharding import PartitionSpec as P

LAYER = ("layer_0", "layer_1")
MESH = pl.DeviceIdType.MESH
B_ROWS, B_CORES = 6, 8


def kernel(
    sizes,
    a_idx,
    a_cnt,
    b_idx,
    b_cnt,
    c_idx,
    c_cnt,
    a_in,
    b_in,
    out,
    a_all,
    a_meta,
    a_tab,
    b_all,
    b_meta,
    b_tab,
    b_hop,
    b_far,
    parts_out,
    parts_in,
    local_sem,
    a_send,
    a_recv,
    m_send,
    m_recv,
    y_send,
    y_recv,
    d_send,
    d_recv,
    h_send,
    h_recv,
    x_send,
    x_recv,
):
    row_count, col_count, x_count = sizes
    y_count = row_count // 2
    z_count = 2 * col_count
    reach = z_count // 2
    half = a_in.shape[1] // 2
    row, col = lax.axis_index("row"), lax.axis_index("col")
    high, x = lax.axis_index("layer_0"), lax.axis_index("layer_1")
    y, core = row // 2, row % 2
    z = high * col_count + col

    def at_z(step):
        there = (z + step + z_count) % z_count
        return {"layer_0": there // col_count, "col": there % col_count}

    def row_at(step, which):
        return ((y + step + y_count) % y_count) * 2 + which

    def at_row(step, which):
        return {"row": row_at(step, which)}

    def at_x(step):
        return {"layer_1": (x + step) % x_count}

    def send(src, dst, send_sem, recv_sem, where):
        copy = pltpu.make_async_remote_copy(
            src_ref=src, dst_ref=dst, send_sem=send_sem, recv_sem=recv_sem, device_id=where, device_id_type=MESH
        )
        copy.start()
        sent.append(copy)

    def arrived(ref, sem):
        pltpu.make_async_copy(ref, ref, sem).wait()

    sent = []

    own_a = pltpu.make_async_copy(a_in, a_all.at[pl.ds(0, 2)], local_sem.at[0])
    own_b = pltpu.make_async_copy(b_in, b_all.at[pl.ds(2 * row, 2)], local_sem.at[1])
    own_a.start()
    own_b.start()
    lane = lax.broadcasted_iota(jnp.int32, (1, 128), 1)
    listed = jnp.zeros((1, 128), jnp.int32)
    for place, value in enumerate((a_idx[0], a_idx[1], a_cnt[0], b_idx[2], b_idx[3], b_cnt[0])):
        listed = jnp.where(lane == place, value, listed)
    a_meta[0] = listed
    b_meta[row] = listed

    barrier = pltpu.get_barrier_semaphore()
    partners = [at_z(1), at_z(-1), at_row(0, 1 - core)]
    partners += [at_row(step, core) for step in range(1, y_count)]
    partners += [at_x(step) for step in range(1, x_count)]
    for partner in partners:
        pl.semaphore_signal(barrier, inc=1, device_id=partner, device_id_type=MESH)
    own_a.wait()
    own_b.wait()
    pl.semaphore_wait(barrier, len(partners))

    def rows_from(step, which):
        return b_all.at[pl.ds(2 * row_at(-step, which), 2)], b_meta.at[row_at(-step, which)]

    def b_over_y():
        tile, lists = rows_from(0, core)
        for step in range(1, y_count):
            send(lists, lists, y_send.at[0, step], y_recv.at[0, step], at_row(step, core))
            send(tile, tile, y_send.at[1, step], y_recv.at[1, step], at_row(step, core))
        send(lists, lists, d_send.at[0, 0], d_recv.at[0, 0], at_row(0, 1 - core))
        send(tile, tile, d_send.at[1, 0], d_recv.at[1, 0], at_row(0, 1 - core))

    def b_over_cores():
        for step in range(1, y_count):
            tile, lists = rows_from(step, core)
            arrived(lists, y_recv.at[0, step])
            arrived(tile, y_recv.at[1, step])
            send(lists, lists, d_send.at[0, step], d_recv.at[0, step], at_row(0, 1 - core))
            send(tile, tile, d_send.at[1, step], d_recv.at[1, step], at_row(0, 1 - core))

    def b_gathered():
        for step in range(y_count):
            tile, lists = rows_from(step, 1 - core)
            arrived(lists, d_recv.at[0, step])
            arrived(tile, d_recv.at[1, step])
        table = pltpu.make_async_copy(b_meta, b_tab, local_sem.at[2])
        table.start()
        table.wait()

    def place_of_b(column):
        place = jnp.int32(0)
        for r in range(row_count):
            for slot in range(2):
                hit = (b_tab[r, 0, 3 + slot] == column) & (slot < b_tab[r, 0, 5])
                place = jnp.where(hit, 2 * r + slot, place)
        return place

    def b_hop_send(hop, side):
        src = b_hop.at[side, hop]
        if hop + 1 < reach:
            dst = b_hop.at[side, hop + 1]
        else:
            dst = b_far.at[row, pl.ds(side * half, half)]
        send(src, dst, h_send.at[side, hop], h_recv.at[side, hop], at_z(1 - 2 * side))

    def b_turn():
        b_gathered()
        block = b_all[place_of_b(row)]
        b_hop[0, 0] = block[:half]
        b_hop[1, 0] = block[half:]
        for side in range(2):
            b_hop_send(0, side)

    def b_forward(hop):
        for side in range(2):
            arrived(b_hop.at[side, hop], h_recv.at[side, hop - 1])
            b_hop_send(hop, side)

    def b_far_over_y():
        for side in range(2):
            arrived(b_far.at[row, pl.ds(side * half, half)], h_recv.at[side, reach - 1])
        block = b_far.at[row]
        for step in range(1, y_count):
            send(block, block, y_send.at[2, step], y_recv.at[2, step], at_row(step, core))
        send(block, block, d_send.at[2, 0], d_recv.at[2, 0], at_row(0, 1 - core))

    def b_far_over_cores():
        for step in range(1, y_count):
            block = b_far.at[row_at(-step, core)]
            arrived(block, y_recv.at[2, step])
            send(block, block, d_send.at[2, step], d_recv.at[2, step], at_row(0, 1 - core))

    def b_far_gathered():
        for step in range(y_count):
            arrived(b_far.at[row_at(-step, 1 - core)], d_recv.at[2, step])

    def a_slot(side, tick):
        step, slot = tick // 2, tick % 2
        if step == reach - 1:
            slot = side
        offset = (z_count - step) % z_count if side == 0 else step
        beyond = z_count - step - 1 if side == 0 else step + 1
        return 2 * offset + slot, 2 * beyond + slot

    def a_tick(tick):
        for side in range(2):
            here, there = a_slot(side, tick)
            if tick >= 2:
                before = tick - 2
                if tick // 2 == reach - 1:
                    before = tick - 2 + side
                arrived(a_all.at[here], a_recv.at[side, before])
                waited.add((side, before))
            send(a_all.at[here], a_all.at[there], a_send.at[side, tick], a_recv.at[side, tick], at_z(1 - 2 * side))

    def lists_step(step):
        for side in range(2):
            offset = (z_count - step) % z_count if side == 0 else step
            beyond = z_count - step - 1 if side == 0 else step + 1
            if step == reach - 1 and side == 1:
                continue
            if step >= 1:
                arrived(a_meta.at[offset], m_recv.at[side, step - 1])
            send(a_meta.at[offset], a_meta.at[beyond], m_send.at[side, step], m_recv.at[side, step], at_z(1 - 2 * side))

    def lists_done():
        last = reach - 1
        arrived(a_meta.at[z_count - last - 1], m_recv.at[0, last])
        if last >= 1:
            arrived(a_meta.at[last], m_recv.at[1, last - 1])
        table = pltpu.make_async_copy(a_meta, a_tab, local_sem.at[3])
        table.start()
        table.wait()

    orders = [step for step in (2, 1, 3) if step < x_count] + [0]
    wanted = []

    def find_blocks():
        slots = []
        for step in orders:
            for slot in range(2):
                s = high * 2 * x_count + 2 * ((x + step) % x_count) + slot
                slots.append((step, slot, c_idx[0, s], c_idx[1, s]))

        def look(o, places):
            in_high = ((z + o) % z_count) // col_count
            other = in_high != high
            places = list(places)
            for which in range(2):
                found = a_tab[o, 0, which]
                live = which < a_tab[o, 0, 2]
                here = 2 * o + which
                for n, (_, _, i, _) in enumerate(slots):
                    hit = live & (found == i)
                    places[2 * n] = jnp.where(hit & jnp.logical_not(other), here, places[2 * n])
                    places[2 * n + 1] = jnp.where(hit & other, here, places[2 * n + 1])
            return tuple(places)

        places = lax.fori_loop(0, z_count, look, (jnp.int32(0),) * (2 * len(slots)))
        for n, (step, slot, _, j) in enumerate(slots):
            wanted.append((step, slot, places[2 * n], places[2 * n + 1], place_of_b(j), j))

    waited = set()
    ticks = 2 * reach - 1
    turn = B_CORES
    stages = [(-1, b_over_y), (B_ROWS, b_over_cores), (B_CORES, b_turn)]
    stages += [(B_CORES + hop, functools.partial(b_forward, hop)) for hop in range(1, reach)]
    stages += [(B_CORES + reach, b_far_over_y)]
    stages += [(B_CORES + reach + 3, b_far_over_cores), (B_CORES + reach + 5, b_far_gathered)]
    stages += [(step, functools.partial(lists_step, step)) for step in range(reach)]
    stages += [(turn + reach, lists_done), (turn + reach + 1, find_blocks)]
    stages.sort(key=lambda pair: pair[0])
    for tick in range(ticks):
        while stages and stages[0][0] < tick:
            stages.pop(0)[1]()
        a_tick(tick)
    for _, stage in stages:
        stage()
    for side in range(2):
        for tick in range(ticks):
            if (side, tick) not in waited:
                arrived(a_all.at[a_slot(side, tick)[1]], a_recv.at[side, tick])

    for step, slot, near, far, b_near, j in wanted:
        total = jnp.dot(a_all[near], b_all[b_near], preferred_element_type=jnp.float32)
        total += jnp.dot(a_all[far], b_far[j], preferred_element_type=jnp.float32)
        if step == 0:
            out[slot] = total
        else:
            parts_out[step, slot] = total.astype(jnp.bfloat16)
        if step != 0 and slot == 1:
            send(parts_out.at[step], parts_in.at[step], x_send.at[step], x_recv.at[step], at_x(step))
    for step in orders[:-1]:
        arrived(parts_in.at[step], x_recv.at[step])
    for slot in range(2):
        total = out[slot]
        for step in range(1, x_count):
            total += parts_in[step, slot].astype(jnp.float32)
        s = high * 2 * x_count + 2 * x + slot
        out[slot] = jnp.where(s < c_cnt[0], total, 0.0)
    for copy in sent:
        copy.wait_send()


def on_device(a_values, a_index, a_count, b_values, b_index, b_count, c_index, c_count):
    row_count, col_count = lax.axis_size("row"), lax.axis_size("col")
    x_count = lax.axis_size("layer_1")
    y_count, z_count = row_count // 2, 2 * col_count
    reach = z_count // 2
    block = a_values.shape[-1]
    dtype = a_values.dtype
    smem = pl.BlockSpec(memory_space=pltpu.SMEM)
    anywhere = pl.BlockSpec(memory_space=pl.ANY)
    vmem = pl.BlockSpec(memory_space=pltpu.VMEM)
    result = pl.pallas_call(
        functools.partial(kernel, (row_count, col_count, x_count)),
        out_shape=jax.ShapeDtypeStruct((2, block, block), jnp.float32),
        in_specs=[smem] * 6 + [anywhere] * 2,
        out_specs=vmem,
        scratch_shapes=[
            pltpu.VMEM((2 * z_count, block, block), dtype),
            pltpu.VMEM((z_count, 1, 128), jnp.int32),
            pltpu.SMEM((z_count, 1, 128), jnp.int32),
            pltpu.VMEM((2 * row_count, block, block), dtype),
            pltpu.VMEM((row_count, 1, 128), jnp.int32),
            pltpu.SMEM((row_count, 1, 128), jnp.int32),
            pltpu.VMEM((2, reach, block // 2, block), dtype),
            pltpu.VMEM((row_count, block, block), dtype),
            pltpu.VMEM((x_count, 2, block, block), dtype),
            pltpu.VMEM((x_count, 2, block, block), dtype),
            pltpu.SemaphoreType.DMA((4,)),
            pltpu.SemaphoreType.DMA((2, 2 * reach)),
            pltpu.SemaphoreType.DMA((2, 2 * reach)),
            pltpu.SemaphoreType.DMA((2, reach)),
            pltpu.SemaphoreType.DMA((2, reach)),
            pltpu.SemaphoreType.DMA((3, y_count)),
            pltpu.SemaphoreType.DMA((3, y_count)),
            pltpu.SemaphoreType.DMA((3, y_count)),
            pltpu.SemaphoreType.DMA((3, y_count)),
            pltpu.SemaphoreType.DMA((2, reach)),
            pltpu.SemaphoreType.DMA((2, reach)),
            pltpu.SemaphoreType.DMA((x_count,)),
            pltpu.SemaphoreType.DMA((x_count,)),
        ],
        compiler_params=pltpu.CompilerParams(
            collective_id=0, has_side_effects=True, vmem_limit_bytes=40 * 1024 * 1024
        ),
    )(
        a_index[0, 0, 0].reshape(-1),
        a_count[0, 0],
        b_index[0, 0, 0].reshape(-1),
        b_count[0, 0],
        c_index[0, 0],
        c_count[0],
        a_values[0, 0, 0],
        b_values[0, 0, 0].transpose(1, 0, 2),
    )
    return result[None, None]


def solution(mesh):
    highs = 2
    split = Mesh(
        mesh.devices.reshape(mesh.shape["row"], mesh.shape["col"], highs, mesh.shape["layer"] // highs),
        ("row", "col", "layer_0", "layer_1"),
    )
    return jax.shard_map(
        on_device,
        mesh=split,
        in_specs=(
            P("row", LAYER, "col", None, None, None),
            P("row", LAYER, "col", None, None),
            P("row", LAYER, "col"),
            P(LAYER, "row", "col", None, None, None),
            P(LAYER, "row", "col", None, None),
            P(LAYER, "row", "col"),
            P("row", "col", None, None),
            P("row", "col"),
        ),
        out_specs=P("row", "col", LAYER, None, None),
        check_vma=False,
    )
```

profile of v0, /device:TPU:8, one launch (start us, length us, event | category | flops | bytes accessed | tf_op | source)
XLA Modules:
  0.0 152.2 jit_solution(13821123666225042684)
XLA Ops:
  1.9 0.0 copy-start.2
  2.0 0.7 copy-done.2
  2.6 0.0 copy-start.3
  2.6 0.1 reshape_squeeze.6.a_idx
  2.7 0.6 copy-done.3
  3.3 0.1 reshape_squeeze.7.b_idx
  3.4 0.0 copy-start
  3.4 1.0 copy.11
  4.4 0.0 copy-start.1
  4.4 0.0 copy-done
  4.4 0.7 copy-done.1
  5.1 146.3 %shard_map.82 = f32[2,256,256]{2,1,0:T(8,128)S(1)} custom-call(s32[4]{0:T(128)S(1)} %reshape_squeeze.6.a_idx, s32[1]{0:T(128)} %bitcast.11.a_cnt, s32[4]{0:T(128)S(1)} %reshape_squeeze.7.b_idx, s32[1]{0:T(128)} %bitcast.12.b_cnt, s32[2,16]{1,0:T(2,128)S(1)} %bitcast.17, s32[1]{0:T(128)} %bitcast.13.c_cnt, bf16[2,256,256]{2,1,0:T(8,128)(2,1)S(1)} %bitcast.16, ...), custom_call_target="tpu_custom_call" | custom-call | tf_op jit(solution)/shard_map/pallas_call | solution.py:300
  151.4 0.8 copy.16
Async XLA Ops:
  1.9 0.7 copy-start.2
  2.6 0.7 copy-start.3
  3.4 1.0 copy-start
  4.4 0.7 copy-start.1
where the time goes:
time: 152 us
  Pallas kernels  146 us (96%)
  local copies, waits for them, and re-layouts  3.92 us (3%)
  between operations  1.98 us (1%)
    pallas_call x1, Pallas kernels, on_device(): pl.pallas_call(functools.partial(kernel, (row_count, col_count, x_count))...  146 us
    unnamed x10, local copies, waits for them, and re-layouts  3.75 us

commit v1 on v0

v1 whole, which is shorter than its diff:
```python
import functools

import jax
import jax.numpy as jnp
from jax import lax
from jax.experimental import pallas as pl
from jax.experimental.pallas import tpu as pltpu
from jax.sharding import Mesh
from jax.sharding import PartitionSpec as P

LAYER = ("layer_0", "layer_1")
MESH = pl.DeviceIdType.MESH
LINKS, RING, LISTS = 40, 12, 6
B_PASS, B_CORES, B_TURN, B_WAY, B_FAR, B_FAR_PASS, B_FAR_CORES, B_FAR_DONE = 4, 7, 9, 14, 19, 22, 25, 27


def kernel(
    sizes,
    a_idx_in,
    a_cnt_in,
    b_idx_in,
    b_cnt_in,
    c_idx_in,
    c_cnt_in,
    a_in,
    b_in,
    out,
    a_idx,
    a_cnt,
    b_idx,
    b_cnt,
    c_idx,
    c_cnt,
    b_raw,
    a_all,
    a_meta,
    a_tab,
    b_all,
    b_meta,
    b_tab,
    b_hop,
    b_far,
    kept,
    parts_out,
    parts_in,
    local_sem,
    send_sem,
    recv_sem,
    ring_send,
    ring_recv,
    list_send,
    list_recv,
):
    row_count, col_count, x_count = sizes
    y_count = row_count // 2
    z_count = 2 * col_count
    reach = z_count // 2
    stride = reach // 2
    half = a_in.shape[1] // 2
    row, col = lax.axis_index("row"), lax.axis_index("col")
    high, x = lax.axis_index("layer_0"), lax.axis_index("layer_1")
    y, core = row // 2, row % 2
    z = high * col_count + col

    def at_z(step):
        there = (z + step + z_count) % z_count
        return {"layer_0": there // col_count, "col": there % col_count}

    def row_at(step, which):
        return ((y + step + y_count) % y_count) * 2 + which

    def at_row(step, which):
        return {"row": row_at(step, which)}

    def at_x(step):
        return {"layer_1": (x + step + x_count) % x_count}

    sent = []

    def send(src, dst, where):
        link = len(sent)
        copy = pltpu.make_async_remote_copy(
            src_ref=src,
            dst_ref=dst,
            send_sem=send_sem.at[link],
            recv_sem=recv_sem.at[link],
            device_id=where,
            device_id_type=MESH,
        )
        copy.start()
        sent.append(copy)
        return link

    def arrived(ref, link):
        pltpu.make_async_copy(ref, ref, recv_sem.at[link]).wait()

    def ring_copy(src, dst, sends, recvs, place, side):
        return pltpu.make_async_remote_copy(
            src_ref=src,
            dst_ref=dst,
            send_sem=sends.at[place],
            recv_sem=recvs.at[place],
            device_id=at_z(1 - 2 * side),
            device_id_type=MESH,
        )

    def ring_send_on(flying, copy, place):
        if place in flying:
            flying[place].wait_send()
        copy.start()
        flying[place] = copy

    def ring_arrived(ref, recvs, place):
        pltpu.make_async_copy(ref, ref, recvs.at[place]).wait()

    loads = [
        pltpu.make_async_copy(src, dst, local_sem.at[n])
        for n, (src, dst) in enumerate(
            (
                (a_in, a_all.at[pl.ds(0, 2)]),
                (a_idx_in, a_idx),
                (a_cnt_in, a_cnt),
                (b_idx_in, b_idx),
                (b_cnt_in, b_cnt),
                (c_idx_in, c_idx),
                (c_cnt_in, c_cnt),
                (b_in, b_raw),
            )
        )
    ]
    for load in loads:
        load.start()
    barrier = pltpu.get_barrier_semaphore()
    partners = [at_z(1), at_z(-1), at_row(0, 1 - core), at_row(1, core), at_row(-1, core), at_x(1), at_x(-1)]
    for partner in partners:
        pl.semaphore_signal(barrier, inc=1, device_id=partner, device_id_type=MESH)
    for load in loads[:-1]:
        load.wait()
    lane = lax.broadcasted_iota(jnp.int32, (1, 128), 1)
    listed = jnp.zeros((1, 128), jnp.int32)
    for place, value in enumerate((a_idx[0, 0], a_idx[0, 1], a_cnt[0, 0], b_idx[1, 0], b_idx[1, 1], b_cnt[0, 0])):
        listed = jnp.where(lane == place, value, listed)
    a_meta[0] = listed
    b_meta[row] = listed
    pl.semaphore_wait(barrier, len(partners))

    a_left, a_flying = set(), {}

    def a_slot(side, tick):
        step, slot = tick // 2, tick % 2
        if step == reach - 1:
            slot = side
        offset = (z_count - step) % z_count if side == 0 else step
        beyond = z_count - step - 1 if side == 0 else step + 1
        return 2 * offset + slot, 2 * beyond + slot

    def a_place(side, tick, part):
        return side * RING + (2 * tick + part) % RING

    def a_tick(tick):
        for part in range(2):
            rows = pl.ds(part * half, half)
            for side in range(2):
                here, there = a_slot(side, tick)
                if tick >= 2:
                    before = tick - 2
                    if tick // 2 == reach - 1:
                        before = tick - 2 + side
                    ring_arrived(a_all.at[here, rows], ring_recv, a_place(side, before, part))
                    a_left.remove((side, before, part))
                place = a_place(side, tick, part)
                copy = ring_copy(a_all.at[here, rows], a_all.at[there, rows], ring_send, ring_recv, place, side)
                ring_send_on(a_flying, copy, place)
                a_left.add((side, tick, part))

    def a_done():
        for side, tick, part in sorted(a_left):
            block = a_all.at[a_slot(side, tick)[1], pl.ds(part * half, half)]
            ring_arrived(block, ring_recv, a_place(side, tick, part))

    lists_flying = {}

    def lists_step(step):
        for side in range(2):
            offset = (z_count - step) % z_count if side == 0 else step
            beyond = z_count - step - 1 if side == 0 else step + 1
            if step >= 1:
                ring_arrived(a_meta.at[offset], list_recv, side * LISTS + (step - 1) % LISTS)
            if step < reach - 1 + (side == 0):
                place = side * LISTS + step % LISTS
                copy = ring_copy(a_meta.at[offset], a_meta.at[beyond], list_send, list_recv, place, side)
                ring_send_on(lists_flying, copy, place)

    def lists_done():
        ring_arrived(a_meta.at[reach], list_recv, (reach - 1) % LISTS)
        table = pltpu.make_async_copy(a_meta, a_tab, local_sem.at[8])
        table.start()
        table.wait()

    def tile_from(step, which):
        return b_all.at[pl.ds(2 * row_at(step, which), 2)]

    def lists_from(step, which):
        return b_meta.at[row_at(step, which)]

    def slot_from(step, which, slot):
        return b_all.at[2 * row_at(step, which) + slot]

    b_links = {}

    def b_over_y():
        loads[-1].wait()
        for slot in range(2):
            b_all[2 * row + slot] = b_raw[:, slot, :]
        tile, lists = tile_from(0, core), lists_from(0, core)
        for step in (1, -1):
            b_links["lists", step] = send(lists, lists, at_row(step, core))
            b_links["tile", step] = send(tile, tile, at_row(step, core))
        b_links["lists", "d", 0] = send(lists, lists, at_row(0, 1 - core))
        b_links["tile", "d", 0] = send(tile, tile, at_row(0, 1 - core))

    def b_pass():
        for step in (1, -1):
            slot = 0 if step == 1 else 1
            tile, lists = tile_from(-step, core), lists_from(-step, core)
            arrived(lists, b_links["lists", step])
            arrived(tile, b_links["tile", step])
            one = slot_from(-step, core, slot)
            b_links["one", step] = send(one, one, at_row(step, core))
            if step == 1:
                b_links["lists", 2] = send(lists, lists, at_row(step, core))
            b_links["lists", "d", -step] = send(lists, lists, at_row(0, 1 - core))
            b_links["tile", "d", -step] = send(tile, tile, at_row(0, 1 - core))

    def b_cores():
        tile, lists = tile_from(2, core), lists_from(2, core)
        arrived(lists, b_links["lists", 2])
        for step in (1, -1):
            arrived(slot_from(2, core, 0 if step == 1 else 1), b_links["one", step])
        b_links["lists", "d", 2] = send(lists, lists, at_row(0, 1 - core))
        b_links["tile", "d", 2] = send(tile, tile, at_row(0, 1 - core))

    def place_of_b(column):
        place = jnp.int32(0)
        for r in range(row_count):
            for slot in range(2):
                hit = (b_tab[r, 0, 3 + slot] == column) & (slot < b_tab[r, 0, 5])
                place = jnp.where(hit, 2 * r + slot, place)
        return place

    def b_turn():
        for step in (0, 1, -1, 2):
            arrived(lists_from(step, 1 - core), b_links["lists", "d", step])
            arrived(tile_from(step, 1 - core), b_links["tile", "d", step])
        table = pltpu.make_async_copy(b_meta, b_tab, local_sem.at[9])
        table.start()
        table.wait()
        block = b_all[place_of_b(row)]
        for side in range(2):
            b_hop[side, 0] = block[side * half : (side + 1) * half]
        for side in range(2):
            b_links["way", side] = send(b_hop.at[side, 0], b_hop.at[side, 1], at_z(stride * (1 - 2 * side)))

    def far_half(step, which, side):
        return b_far.at[row_at(step, which), pl.ds(side * half, half)]

    def b_way():
        for side in range(2):
            arrived(b_hop.at[side, 1], b_links["way", side])
            b_links["far", side] = send(
                b_hop.at[side, 1], far_half(0, core, side), at_z((reach - stride) * (1 - 2 * side))
            )

    def b_far_over_y():
        block = b_far.at[row]
        for side in range(2):
            arrived(far_half(0, core, side), b_links["far", side])
        for step in (1, -1):
            b_links["block", step] = send(block, block, at_row(step, core))
        b_links["block", "d", 0] = send(block, block, at_row(0, 1 - core))

    def b_far_pass():
        for step in (1, -1):
            block, one = b_far.at[row_at(-step, core)], far_half(-step, core, 0 if step == 1 else 1)
            arrived(block, b_links["block", step])
            b_links["part", step] = send(one, one, at_row(step, core))
            b_links["block", "d", -step] = send(block, block, at_row(0, 1 - core))

    def b_far_cores():
        for step in (1, -1):
            arrived(far_half(2, core, 0 if step == 1 else 1), b_links["part", step])
        block = b_far.at[row_at(2, core)]
        b_links["block", "d", 2] = send(block, block, at_row(0, 1 - core))

    def b_far_done():
        for step in (0, 1, -1, 2):
            arrived(b_far.at[row_at(step, 1 - core)], b_links["block", "d", step])

    wanted = {}

    def find_blocks():
        slots = []
        for step in range(x_count):
            for slot in range(2):
                s = high * 2 * x_count + 2 * ((x + step) % x_count) + slot
                slots.append((step, slot, c_idx[0, s], c_idx[1, s]))

        def look(o, places):
            other = ((z + o) % z_count) // col_count != high
            places = list(places)
            for which in range(2):
                found = a_tab[o, 0, which]
                live = which < a_tab[o, 0, 2]
                here = 2 * o + which
                for n, (_, _, i, _) in enumerate(slots):
                    hit = live & (found == i)
                    places[2 * n] = jnp.where(hit & jnp.logical_not(other), here, places[2 * n])
                    places[2 * n + 1] = jnp.where(hit & other, here, places[2 * n + 1])
            return tuple(places)

        places = lax.fori_loop(0, z_count, look, (jnp.int32(0),) * (2 * len(slots)))
        for n, (step, slot, _, j) in enumerate(slots):
            wanted[step, slot] = (places[2 * n], places[2 * n + 1], place_of_b(j), j)

    def product(step, slot):
        near, far, b_near, j = wanted[step, slot]
        total = jnp.dot(a_all[near], b_all[b_near], preferred_element_type=jnp.float32)
        return total + jnp.dot(a_all[far], b_far[j], preferred_element_type=jnp.float32)

    stages = [(0, b_over_y), (B_PASS, b_pass), (B_CORES, b_cores), (B_TURN, b_turn), (B_WAY, b_way)]
    stages += [(B_FAR, b_far_over_y), (B_FAR_PASS, b_far_pass), (B_FAR_CORES, b_far_cores), (B_FAR_DONE, b_far_done)]
    stages += [(step, functools.partial(lists_step, step)) for step in range(reach)]
    stages += [(B_TURN + reach, lists_done), (B_TURN + reach + 1, find_blocks)]
    stages.sort(key=lambda pair: pair[0])
    for tick in range(2 * reach - 1):
        a_tick(tick)
        while stages and stages[0][0] <= tick:
            stages.pop(0)[1]()
    for _, stage in stages:
        stage()
    a_done()

    def pass_on(n, value, step):
        parts_out[n] = value.astype(jnp.bfloat16)
        return send(parts_out.at[n], parts_in.at[n], at_x(step))

    def taken(n, link):
        arrived(parts_in.at[n], link)
        return parts_in[n].astype(jnp.float32)

    up = pass_on(0, product(2, 0), 1)
    down = pass_on(1, product(2, 1), -1)
    below = pass_on(2, product(1, 1), 1)
    above = pass_on(3, product(3, 0), -1)
    kept[0] = product(1, 0)
    kept[1] = product(3, 1)
    out[0] = product(0, 0)
    out[1] = product(0, 1)
    up = pass_on(4, kept[0] + taken(0, up), 1)
    down = pass_on(5, kept[1] + taken(1, down), -1)
    out[1] += taken(2, below)
    out[0] += taken(3, above)
    for slot, (n, link) in enumerate(((4, up), (5, down))):
        s = high * 2 * x_count + 2 * x + slot
        out[slot] = jnp.where(s < c_cnt[0, 0], out[slot] + taken(n, link), 0.0)
    for copy in [*sent, *a_flying.values(), *lists_flying.values()]:
        copy.wait_send()


def on_device(a_values, a_index, a_count, b_values, b_index, b_count, c_index, c_count):
    row_count, col_count = lax.axis_size("row"), lax.axis_size("col")
    x_count = lax.axis_size("layer_1")
    assert row_count == 8 and x_count == 4
    z_count = 2 * col_count
    block = a_values.shape[-1]
    dtype = a_values.dtype
    far_memory = pl.BlockSpec(memory_space=pltpu.HBM)
    vmem = pl.BlockSpec(memory_space=pltpu.VMEM)
    lists = (
        a_index[0, 0, 0],
        a_count[0, 0][None],
        b_index[0, 0, 0],
        b_count[0, 0][None],
        c_index[0, 0],
        c_count,
    )
    result = pl.pallas_call(
        functools.partial(kernel, (row_count, col_count, x_count)),
        out_shape=jax.ShapeDtypeStruct((2, block, block), jnp.float32),
        in_specs=[far_memory] * 8,
        out_specs=vmem,
        scratch_shapes=[pltpu.SMEM(x.shape, jnp.int32) for x in lists]
        + [
            pltpu.VMEM((block, 2, block), dtype),
            pltpu.VMEM((2 * z_count, block, block), dtype),
            pltpu.VMEM((z_count, 1, 128), jnp.int32),
            pltpu.SMEM((z_count, 1, 128), jnp.int32),
            pltpu.VMEM((2 * row_count, block, block), dtype),
            pltpu.VMEM((row_count, 1, 128), jnp.int32),
            pltpu.SMEM((row_count, 1, 128), jnp.int32),
            pltpu.VMEM((2, 2, block // 2, block), dtype),
            pltpu.VMEM((row_count, block, block), dtype),
            pltpu.VMEM((2, block, block), jnp.float32),
            pltpu.VMEM((6, block, block), dtype),
            pltpu.VMEM((6, block, block), dtype),
            pltpu.SemaphoreType.DMA((10,)),
            pltpu.SemaphoreType.DMA((LINKS,)),
            pltpu.SemaphoreType.DMA((LINKS,)),
            pltpu.SemaphoreType.DMA((2 * RING,)),
            pltpu.SemaphoreType.DMA((2 * RING,)),
            pltpu.SemaphoreType.DMA((2 * LISTS,)),
            pltpu.SemaphoreType.DMA((2 * LISTS,)),
        ],
        compiler_params=pltpu.CompilerParams(
            collective_id=0, has_side_effects=True, vmem_limit_bytes=40 * 1024 * 1024
        ),
    )(*lists, a_values[0, 0, 0], b_values[0, 0, 0])
    return result[None, None]


def solution(mesh):
    highs = 2
    split = Mesh(
        mesh.devices.reshape(mesh.shape["row"], mesh.shape["col"], highs, mesh.shape["layer"] // highs),
        ("row", "col", "layer_0", "layer_1"),
    )
    return jax.shard_map(
        on_device,
        mesh=split,
        in_specs=(
            P("row", LAYER, "col", None, None, None),
            P("row", LAYER, "col", None, None),
            P("row", LAYER, "col"),
            P(LAYER, "row", "col", None, None, None),
            P(LAYER, "row", "col", None, None),
            P(LAYER, "row", "col"),
            P("row", "col", None, None),
            P("row", "col"),
        ),
        out_specs=P("row", "col", LAYER, None, None),
        check_vma=False,
    )
```

time: 152 us -> 149 us (0.980)
  the two profiles are of different devices: /device:TPU:8 before, /device:TPU:2 now
where the time goes in v1:
time: 149 us
  Pallas kernels  144 us (97%)
  local copies, waits for them, and re-layouts  3.38 us (2%)
  between operations  1.98 us (1%)
    pallas_call x1, Pallas kernels, on_device(): pl.pallas_call(functools.partial(kernel, (row_count, col_count, x_count))...  144 us
    unnamed x11, local copies, waits for them, and re-layouts  3.38 us

profile of v1, /device:TPU:2, one launch (start us, length us, event | category | flops | bytes accessed | tf_op | source)
XLA Modules:
  0.0 149.0 jit_solution(3352171340023353635)
XLA Ops:
  1.9 0.0 copy-start.3
  2.0 0.0 copy-start.4
  2.0 0.0 copy-start.2
  2.0 0.7 copy-done.3
  2.6 0.0 copy-done.4
  2.6 0.0 copy-done.2
  2.7 0.0 copy-start
  2.7 0.9 copy-done
  3.6 0.0 copy-start.1
  3.6 0.9 copy-done.1
  4.6 143.7 %shard_map.82 = f32[2,256,256]{2,1,0:T(8,128)S(1)} custom-call(s32[2,2]{1,0:T(2,128)S(1)} %bitcast.13, s32[1,1]{1,0:T(1,128)} %bitcast.8.a_cnt_in, s32[2,2]{1,0:T(2,128)S(1)} %bitcast.14, s32[1,1]{1,0:T(1,128)} %bitcast.9.b_cnt_in, s32[2,16]{1,0:T(2,128)S(1)} %bitcast.15, s32[1,1]{1,0:T(1,128)S(6)} %copy.12.c_cnt_in, bf16[2,256,256]{2,1,0:T(8,128)(2,1)S(1)} %bitcast.11, ...), custom_call_target="tpu_custom_call" | custom-call | tf_op jit(solution)/shard_map/pallas_call | solution.py:387
  148.2 0.8 copy.13
Async XLA Ops:
  1.9 0.7 copy-start.3
  2.0 0.7 copy-start.4
  2.0 0.7 copy-start.2
  2.7 0.9 copy-start
  3.6 0.9 copy-start.1

commit v2 on v1

--- a/solution.py
+++ b/solution.py
@@ -10,7 +10,7 @@
 
 LAYER = ("layer_0", "layer_1")
 MESH = pl.DeviceIdType.MESH
-LINKS, RING, LISTS = 40, 12, 6
+LINKS, RING, LISTS = 48, 12, 6
 B_PASS, B_CORES, B_TURN, B_WAY, B_FAR, B_FAR_PASS, B_FAR_CORES, B_FAR_DONE = 4, 7, 9, 14, 19, 22, 25, 27
 
 
@@ -248,6 +248,28 @@
                 place = jnp.where(hit, 2 * r + slot, place)
         return place
 
+    third = 3 * a_in.shape[1] // 8
+    up_rows, down_rows = pl.ds(0, third), pl.ds(third, third)
+    mid_rows = pl.ds(2 * third, a_in.shape[1] - 2 * third)
+    relays = (z >= stride) & (z < 3 * stride)
+    mid_send, mid_up, mid_down, relay_up, relay_down, mid_far = range(LINKS - 6, LINKS)
+
+    def mid_copy(src, dst, step, send_link, recv_link):
+        return pltpu.make_async_remote_copy(
+            src_ref=src,
+            dst_ref=dst,
+            send_sem=send_sem.at[send_link],
+            recv_sem=recv_sem.at[recv_link],
+            device_id=at_z(step),
+            device_id_type=MESH,
+        )
+
+    def mid_relays():
+        return (
+            mid_copy(b_hop.at[1, mid_rows], b_far.at[row, mid_rows], reach - stride, relay_up, mid_far),
+            mid_copy(b_hop.at[2, mid_rows], b_far.at[row, mid_rows], stride - reach, relay_down, mid_far),
+        )
+
     def b_turn():
         for step in (0, 1, -1, 2):
             arrived(lists_from(step, 1 - core), b_links["lists", "d", step])
@@ -255,26 +277,39 @@
         table = pltpu.make_async_copy(b_meta, b_tab, local_sem.at[9])
         table.start()
         table.wait()
-        block = b_all[place_of_b(row)]
-        for side in range(2):
-            b_hop[side, 0] = block[side * half : (side + 1) * half]
-        for side in range(2):
-            b_links["way", side] = send(b_hop.at[side, 0], b_hop.at[side, 1], at_z(stride * (1 - 2 * side)))
+        b_hop[0] = b_all[place_of_b(row)]
+        b_links["way", 0] = send(b_hop.at[0, up_rows], b_hop.at[1, up_rows], at_z(stride))
+        b_links["way", 1] = send(b_hop.at[0, down_rows], b_hop.at[1, down_rows], at_z(-stride))
+
+        @pl.when(high == 0)
+        def _():
+            mid_copy(b_hop.at[0, mid_rows], b_hop.at[1, mid_rows], stride, mid_send, mid_up).start()
+
+        @pl.when(high == 1)
+        def _():
+            mid_copy(b_hop.at[0, mid_rows], b_hop.at[2, mid_rows], -stride, mid_send, mid_down).start()
 
     def far_half(step, which, side):
         return b_far.at[row_at(step, which), pl.ds(side * half, half)]
 
     def b_way():
-        for side in range(2):
-            arrived(b_hop.at[side, 1], b_links["way", side])
-            b_links["far", side] = send(
-                b_hop.at[side, 1], far_half(0, core, side), at_z((reach - stride) * (1 - 2 * side))
-            )
+        for side, rows in enumerate((up_rows, down_rows)):
+            arrived(b_hop.at[1, rows], b_links["way", side])
+            step = (reach - stride) * (1 - 2 * side)
+            b_links["far", side] = send(b_hop.at[1, rows], b_far.at[row, rows], at_z(step))
+
+        @pl.when(relays)
+        def _():
+            arrived(b_hop.at[1, mid_rows], mid_up)
+            arrived(b_hop.at[2, mid_rows], mid_down)
+            for copy in mid_relays():
+                copy.start()
 
     def b_far_over_y():
         block = b_far.at[row]
-        for side in range(2):
-            arrived(far_half(0, core, side), b_links["far", side])
+        for side, rows in enumerate((up_rows, down_rows)):
+            arrived(b_far.at[row, rows], b_links["far", side])
+        arrived(b_far.at[row, mid_rows], mid_far)
         for step in (1, -1):
             b_links["block", step] = send(block, block, at_row(step, core))
         b_links["block", "d", 0] = send(block, block, at_row(0, 1 - core))
@@ -365,6 +400,13 @@
         out[slot] = jnp.where(s < c_cnt[0, 0], out[slot] + taken(n, link), 0.0)
     for copy in [*sent, *a_flying.values(), *lists_flying.values()]:
         copy.wait_send()
+    mid = b_hop.at[0, mid_rows]
+    pltpu.make_async_copy(mid, mid, send_sem.at[mid_send]).wait()
+
+    @pl.when(relays)
+    def _():
+        for copy in mid_relays():
+            copy.wait_send()
 
 
 def on_device(a_values, a_index, a_count, b_values, b_index, b_count, c_index, c_count):
@@ -398,7 +440,7 @@
             pltpu.VMEM((2 * row_count, block, block), dtype),
             pltpu.VMEM((row_count, 1, 128), jnp.int32),
             pltpu.SMEM((row_count, 1, 128), jnp.int32),
-            pltpu.VMEM((2, 2, block // 2, block), dtype),
+            pltpu.VMEM((3, block, block), dtype),
             pltpu.VMEM((row_count, block, block), dtype),
             pltpu.VMEM((2, block, block), jnp.float32),
             pltpu.VMEM((6, block, block), dtype),
@@ -412,7 +454,7 @@
             pltpu.SemaphoreType.DMA((2 * LISTS,)),
         ],
         compiler_params=pltpu.CompilerParams(
-            collective_id=0, has_side_effects=True, vmem_limit_bytes=40 * 1024 * 1024
+            collective_id=0, has_side_effects=True, vmem_limit_bytes=67043328
         ),
     )(*lists, a_values[0, 0, 0], b_values[0, 0, 0])
     return result[None, None]

time: 149 us -> 146 us (0.980)
  the two profiles are of different devices: /device:TPU:2 before, /device:TPU:32 now
where the time goes in v2:
time: 146 us; the launch traced here: 145 us
  Pallas kernels  142 us (97%)
  between operations  1.95 us (1%)
  local copies, waits for them, and re-layouts  1.87 us (1%)
    pallas_call x1, Pallas kernels, on_device(): pl.pallas_call(functools.partial(kernel, (row_count, col_count, x_count))...  142 us

profile of v2, /device:TPU:32, one launch (start us, length us, event | category | flops | bytes accessed | tf_op | source)
XLA Modules:
  0.0 145.4 jit_solution(10590798105979060405)
XLA Ops:
  1.9 141.6 %shard_map.82 = f32[2,256,256]{2,1,0:T(8,128)} custom-call(s32[2,2]{1,0:T(2,128)} %bitcast.13, s32[1,1]{1,0:T(1,128)} %bitcast.8.a_cnt_in, s32[2,2]{1,0:T(2,128)} %bitcast.14, s32[1,1]{1,0:T(1,128)} %bitcast.9.b_cnt_in, s32[2,16]{1,0:T(2,128)} %bitcast.15, s32[1,1]{1,0:T(1,128)S(6)} %copy.12.c_cnt_in, bf16[2,256,256]{2,1,0:T(8,128)(2,1)} %bitcast.11, ...), custom_call_target="tpu_custom_call" | custom-call | tf_op jit(solution)/shard_map/pallas_call | solution.py:429
  143.5 1.9 %copy.13 = f32[1,1,2,256,256]{4,3,2,1,0:T(8,128)} copy(f32[1,1,2,256,256]{4,3,2,1,0:T(8,128)} %bitcast.10) | data formatting | bytes 1048576

commit v3 on v2

--- a/solution.py
+++ b/solution.py
@@ -454,9 +454,12 @@
             pltpu.SemaphoreType.DMA((2 * LISTS,)),
         ],
         compiler_params=pltpu.CompilerParams(
-            collective_id=0, has_side_effects=True, vmem_limit_bytes=67043328
+            collective_id=0, has_side_effects=True, vmem_limit_bytes=40 * 1024 * 1024
         ),
-    )(*lists, a_values[0, 0, 0], b_values[0, 0, 0])
+    )(
+        *(pltpu.with_memory_space_constraint(v, pltpu.HBM) if v.size > 1 else v for v in lists),
+        *(pltpu.with_memory_space_constraint(v[0, 0, 0], pltpu.HBM) for v in (a_values, b_values)),
+    )
     return result[None, None]
 
 

time: 146 us -> 144 us (0.986)
  no operation moved by 1% of the time
where the time goes in v3:
time: 144 us
  Pallas kernels  141 us (98%)
  between operations  1.95 us (1%)
    pallas_call x1, Pallas kernels, on_device(): pl.pallas_call(functools.partial(kernel, (row_count, col_count, x_count))...  141 us

profile of v3, /device:TPU:32, one launch (start us, length us, event | category | flops | bytes accessed | tf_op | source)
XLA Modules:
  0.0 143.5 jit_solution(2245208830121550040)
XLA Ops:
  1.9 140.8 %shard_map.82 = f32[2,256,256]{2,1,0:T(8,128)S(1)} custom-call(s32[2,2]{1,0:T(2,128)} %bitcast.13, s32[1,1]{1,0:T(1,128)} %bitcast.8.a_cnt_in, s32[2,2]{1,0:T(2,128)} %bitcast.14, s32[1,1]{1,0:T(1,128)} %bitcast.9.b_cnt_in, s32[2,16]{1,0:T(2,128)} %bitcast.15, s32[1,1]{1,0:T(1,128)S(6)} %copy.12.c_cnt_in, bf16[2,256,256]{2,1,0:T(8,128)(2,1)} %bitcast.11, ...), custom_call_target="tpu_custom_call" | custom-call | tf_op jit(solution)/shard_map/pallas_call | solution.py:429
  142.7 0.8 copy.13
